TPU v7x, 256 devices: a whole 4x4x8 slice. The times are simulated.
256 devices in a mesh: leaf: 4 (over y_hi, core), grid: 64 (over z, x, y_lo).
Axes of the slice: x: 4, y: 4 (y_hi: 2, y_lo: 2; y = y_hi * 2 + y_lo), z: 8, core: 2. Of those that a mesh axis runs over, the one named last changes fastest.
Arguments:
- ainv_sep: bfloat16 [4, 16384, 16384], P('leaf', 'grid'), may hold values from -6 to 6
- l_panel: bfloat16 [4, 16384, 512], P('leaf', 'grid'), may hold values from -0.046875 to 0.046875
- block_mask: int32 [4, 1, 32], P('leaf'), may hold values 0 or 1
- owner: int32 [4, 32], P('leaf'), may hold values 0 or 1
- dinv: float32 [4, 512, 512], P('leaf', 'grid'), may hold values from -6 to 6
Outputs:
- ainv_panel: bfloat16 [4, 16384, 512], P('leaf', 'grid')
- ainv_upper: bfloat16 [4, 512, 16384], P('leaf', 'grid')
- ainv_diag: float32 [4, 512, 512], P('leaf', 'grid')
All inputs are finite; a program needn't handle non-finite values. No bound on the sum of `block_mask` or of `owner` on one device may be relied on, other than what follows from the above.
Results may differ from a plain program's by a relative error of at most 0.0019.
Values may be sent and summed in bfloat16 or wider, within the bound.
A program may use at most 128 MiB of HBM per device.

v0:
```python
import jax
import jax.numpy as jnp
from jax import lax
from jax.sharding import Mesh
from jax.sharding import PartitionSpec as P

B = 512
GRID = ("grid_0", "grid_1", "grid_2")


def swapped(array, axis, stride):
    return lax.ppermute(array, axis, [(i, i ^ 1 << stride) for i in range(lax.axis_size(axis))])


def in_order(tiles, dim):
    tiles = jnp.moveaxis(tiles, 0, dim)
    lengths = tiles.shape
    return tiles.reshape(*lengths[:dim], lengths[dim] * lengths[dim + 1], *lengths[dim + 2 :])


def gather_in_order(array, axes, turns):
    tiles = array
    for k in turns:
        tiles = lax.all_gather(tiles, axes[k])
    done = turns[::-1]
    back = [done.index(k) for k in range(len(axes))]
    tiles = tiles.transpose(*back, *range(len(axes), tiles.ndim))
    return tiles.reshape(-1, *array.shape)


def gather_axes(array, axes, turns, dim):
    return in_order(gather_in_order(array, axes, turns), dim)


def body(ainv_sep, l_panel, block_mask, owner, dinv):
    strip_rows = ainv_sep.shape[1]
    block_count = block_mask.shape[2]
    sibling = swapped(ainv_sep, "leaf", 0)
    colmask = jnp.repeat(owner[0], B)
    mixed = jnp.where(colmask[None, :] == 1, sibling[0], ainv_sep[0])
    first_row = lax.axis_index(GRID) * strip_rows
    row_block = (first_row + jnp.arange(strip_rows, dtype=jnp.int32)) // B
    onehot = (row_block[:, None] == jnp.arange(block_count, dtype=jnp.int32)[None, :]).astype(
        jnp.float32
    )
    row_flags = jnp.dot(
        onehot, block_mask[0].T.astype(jnp.float32), preferred_element_type=jnp.float32
    )
    flags_wide = jnp.repeat(row_flags, B, axis=1)
    masked = jnp.where(flags_wide > 0.5, l_panel[0], jnp.zeros((), jnp.bfloat16))
    whole_panel = gather_axes(masked, GRID, (2, 0, 1), 0)
    panel = (-jnp.dot(mixed, whole_panel, preferred_element_type=jnp.float32)).astype(jnp.bfloat16)
    upper = lax.all_to_all(panel.T, GRID, split_axis=0, concat_axis=1, tiled=True)
    diag = dinv[0] - jnp.dot(upper, whole_panel, preferred_element_type=jnp.float32)
    return (panel[None], upper[None], diag[None])


def solution(mesh):
    torus = Mesh(
        mesh.devices.reshape(mesh.shape["leaf"], 8, 4, 2), ("leaf", "grid_0", "grid_1", "grid_2")
    )
    placed = (
        P("leaf", GRID, None),
        P("leaf", GRID, None),
        P("leaf", None, None),
        P("leaf", None),
        P("leaf", GRID, None),
    )
    return jax.shard_map(
        body,
        mesh=torus,
        in_specs=placed,
        out_specs=(P("leaf", GRID, None), P("leaf", GRID, None), P("leaf", GRID, None)),
        check_vma=False,
    )
```

profile of v0, /device:TPU:8, one launch (start us, length us, event | category | flops | bytes accessed | tf_op | source)
XLA Modules:
  0.0 301.4 jit_solution(16194278294243282166)
XLA Ops:
  7.2 0.0 all-gather.5.cloned.1.call-start
  7.2 0.9 fusion.11
  8.1 1.1 broadcast_select_fusion
  9.2 8.8 %all_gather.16 = bf16[2,256,512]{2,1,0:T(8,128)(2,1)} all-gather(bf16[1,256,512]{2,1,0:T(8,128)(2,1)S(1)} %broadcast_select_fusion), channel_id=1, replica_groups=mesh['leaf'=4,'grid_0'=8,'grid_1'=4,'grid_2'=2] {'grid_2'}, dimensions={0}, use_global_device_ids=true | all-gather | bytes 786432 | tf_op jit(solution)/shard_map/all_gather | solution.py:24
  18.0 0.0 all-gather.5.cloned.1.call-update
  18.0 0.0 all-gather.7.cloned.1.call-start
  18.1 57.7 %all-gather.5.cloned.1.call-done = bf16[16,256,512]{2,1,0:T(8,128)(2,1)} async-done(((bf16[2,256,512]{2,1,0:T(8,128)(2,1)}), bf16[16,256,512]{2,1,0:T(8,128)(2,1)}) %all-gather.5.cloned.1.call-update) | async-done | bytes 4194320 | tf_op jit(solution)/shard_map/all_gather | solution.py:24
  75.8 0.0 all-gather.7.cloned.1.call-update
  75.8 0.1 collective-permute-start
  75.9 0.7 compare_bitcast_fusion
  76.6 0.1 broadcast_bitcast_fusion
  76.7 156.1 %all-gather.7.cloned.1.call-done = bf16[32,2,256,512]{3,2,1,0:T(8,128)(2,1)} async-done(((bf16[8,2,256,512]{3,2,1,0:T(8,128)(2,1)}), bf16[32,2,256,512]{3,2,1,0:T(8,128)(2,1)}) %all-gather.7.cloned.1.call-update) | async-done | bytes 16777232 | tf_op jit(solution)/shard_map/all_gather | solution.py:24
  232.8 13.7 %copy.12 = bf16[8,4,2,256,512]{4,3,2,1,0:T(8,128)(2,1)} copy(bf16[8,4,2,256,512]{4,3,2,0,1:T(8,128)(2,1)} %bitcast.40) | data formatting | bytes 33554432 | tf_op jit(solution)/shard_map/transpose | solution.py:27
  246.5 0.0 collective-permute-done
  246.5 0.0 copy-start.1
  246.5 15.0 %fusion.7 = bf16[256,512]{1,0:T(8,128)(2,1)S(1)} fusion(bf16[16384,512]{1,0:T(8,128)(2,1)} %bitcast.38, bf16[1,256,16384]{2,1,0:T(8,128)(2,1)} %collective-permute-done, bf16[1,256,16384]{2,1,0:T(8,128)(2,1)} %param.5, pred[16384]{0:T(1024)(128)(4,1)S(1)} %bitcast.47), kind=kOutput, calls=%fused_computation.5 | convolution fusion | flops 4299423744 | bytes 33832960 | tf_op jit(solution)/shard_map/dot_general | solution.py:52
  261.6 0.0 copy-start
  261.6 0.1 copy.13
  261.7 23.5 %all_to_all.19 = bf16[64,8,256]{2,1,0:T(8,128)(2,1)S(1)} all-to-all(bf16[64,8,256]{2,1,0:T(8,128)(2,1)S(1)} %bitcast.44), channel_id=1, replica_groups=mesh['leaf'=4,'grid_0'=8,'grid_1'=4,'grid_2'=2] {'grid_0','grid_1','grid..., dimensions={0} | all-to-all | bytes 524288 | tf_op jit(solution)/shard_map/all_to_all | solution.py:53
  285.2 0.0 copy-done.1
  285.2 8.6 %fusion.10 = f32[1,8,512]{2,1,0:T(8,128)} fusion(bf16[8,16384]{1,0:T(8,128)(2,1)S(1)} %bitcast.42, bf16[16384,512]{1,0:T(8,128)(2,1)} %bitcast.39, f32[1,8,512]{2,1,0:T(8,128)S(1)} %copy-done.1), kind=kOutput, calls=%fused_computation.7 | convolution fusion | flops 134221824 | bytes 17072128 | tf_op jit(solution)/shard_map/dot_general | solution.py:54
  293.8 0.0 copy-done
  293.8 0.7 copy.16
  (3 shorter events, 0.0 us)
Async XLA Ops:
  7.2 68.6 %all-gather.5.cloned.1.call-start = ((), (), s32[]{:S(2)}) async-start(), calls=%async_computation.1 | async-start | bytes 4718592 | tf_op jit(solution)/shard_map/all_gather | solution.py:24
  18.0 214.8 %all-gather.7.cloned.1.call-start = ((), (), s32[]{:S(2)}) async-start(), calls=%async_computation.2 | async-start | bytes 20971520 | tf_op jit(solution)/shard_map/all_gather | solution.py:24
  75.8 170.7 %collective-permute-start = (bf16[1,256,16384]{2,1,0:T(8,128)(2,1)}, bf16[1,256,16384]{2,1,0:T(8,128)(2,1)}, u32[]{:S(2)}, u32[]{:S(2)}) collective-permute-start(bf16[1,256,16384]{2,1,0:T(8,128)(2,1)} %param.5), channel_id=1, source_target_pairs={{0,64},{64,0},{128,192},{192,128},{1,65},{65,1},{129,193},{193,129... | collective-permute-start | bytes 25165832 | tf_op jit(solution)/shard_map/ppermute | solution.py:12
  246.5 38.7 %copy-start.1 = (f32[1,8,512]{2,1,0:T(8,128)S(1)}, f32[1,8,512]{2,1,0:T(8,128)}, u32[]{:S(2)}) copy-start(f32[1,8,512]{2,1,0:T(8,128)} %param.9) | copy-start | bytes 49156
  261.6 32.3 %copy-start = (bf16[256,512]{1,0:T(8,128)(2,1)}, bf16[256,512]{1,0:T(8,128)(2,1)S(1)}, u32[]{:S(2)}) copy-start(bf16[256,512]{1,0:T(8,128)(2,1)S(1)} %fusion.7) | copy-start | bytes 786436
Sparse Core Ops, SparseCore 0:
  18.1 57.6 all-gather.4
  77.6 155.1 all-gather.6
where the time goes:
time: 302 us; the launch traced here: 301 us
  waiting for transfers between devices  214 us (71%)
  blocking collectives  32.3 us (11%)
  matrix products  24.5 us (8%)
  local copies, waits for them, and re-layouts  14.7 us (5%)
  between operations  14.1 us (5%)
    all_gather x2, waiting for transfers between devices, gather_in_order(): tiles = lax.all_gather(tiles, axes[k])  214 us
    all_to_all x1, blocking collectives, body(): lax.all_to_all(panel.T, GRID, split_axis=0, concat_axis=1, tiled=True)  23.5 us
    dot_general x1, matrix products, body(): jnp.dot(mixed, whole_panel, preferred_element_type=jnp.float32)  15 us
    transpose x1, local copies, waits for them, and re-layouts, gather_in_order(): tiles = tiles.transpose(*back, *range(len(axes), tiles.ndim))  13.7 us
    all_gather x1, blocking collectives, gather_in_order(): tiles = lax.all_gather(tiles, axes[k])  8.82 us
    dot_general x1, matrix products, body(): jnp.dot(upper, whole_panel, preferred_element_type=jnp.float32)  8.65 us
  transfers between devices with their start and end apart: 3, of which 2 were waited for; matrix products, arithmetic and copies ran while one was open for 5% of the time, Pallas kernels for 0%

commit v1 on v0

v1 whole, which is shorter than its diff:
```python
import functools

import jax
import jax.numpy as jnp
from jax import lax
from jax.experimental import pallas as pl
from jax.experimental.pallas import tpu as pltpu
from jax.sharding import PartitionSpec as P

MESH = pl.DeviceIdType.MESH
B = 512
SEP = 16384
ROWS = 256
NZ, NX, NY = 8, 4, 2
NGRID = NZ * NX * NY
LENGTH = {"z": NZ, "x": NX, "y": NY}

FIRST = (0, 80, 160)
COUNT = (80, 80, 96)
AXES = ("yxz", "yzx", "zxy")
OWN_ORDER = {"z": (2, 1, 0), "x": (0, 2, 1), "y": (0, 1, 2)}

EVENTS = (
    10, 201, 202, 27000, 21000, 10010, 20201, 20202, 17000, 11000, 20010, 7000, 1000, 10202,
    10201, 7010, 1010, 212, 211, 27010, 200, 21010, 7100, 7300, 1100, 1300, 27201, 27202,
    21201, 21202, 20310, 20110, 26000, 22000, 10212, 10211, 17010, 11010, 20200, 16000, 12000, 17201,
    17202, 27110, 27310, 6000, 2000, 11201, 11202, 6010, 2010, 210, 10200, 21110, 21310, 27200,
    7310, 7110, 1310, 1110, 21200, 26201, 26010, 1200, 7200, 26202, 22201, 22010, 6100, 2100,
    10210, 22202, 6300, 2300, 20210, 17212, 17211, 27210, 24001, 24002, 11211, 11212, 16010, 12010,
    16201, 16202, 21210, 14001, 14002, 12201, 12202, 4002, 4001, 26310, 26110, 17200, 26200, 4011,
    4012, 11200, 17210, 1210, 7210, 22200, 22310, 22110, 6310, 2310, 23201, 25201, 2110, 6110,
    23202, 25202, 11210, 23010, 25010, 2200, 6200, 12212, 12211, 4101, 4102, 26210, 16212, 16211,
    4301, 4302, 16200, 22210, 24000, 15201, 13201, 14011, 14012, 15202, 13202, 14000, 4000, 4010,
    23310, 23110, 23200, 12200, 16210, 6210, 2210, 25310, 25110, 25200, 12210, 4311, 4312, 4111,
    4112, 24201, 24202, 24010, 4202, 4201, 15200, 25210, 4100, 13200, 15211, 13211, 14010, 4212,
    4300, 23210, 4310, 13212, 15212, 14201, 4110, 4211, 14202, 24310, 24110, 4200, 24200, 13210,
    4210, 15210, 14211, 14212, 24210, 14200, 14210,
)
SITES = {
    36: (0, 1, 3, 28,),
    76: (4, 2, 29, 31,),
    83: (5, 7, 24, 8,),
    120: (30, 6, 9, 11,),
    134: (25, 27, 12, 20,),
    171: (26, 10, 16, 13,),
    181: (15, 21, 23, 14,),
    188: (22, 17, 19, 18,),
}


def decode(event):
    return event // 10000, event // 1000 % 10, event // 100 % 10, event // 10 % 10, event % 10


def last_axis(piece, offset):
    moved = [axis for axis in AXES[piece] if offset[axis]]
    return moved[-1] if moved else None


def side(piece, axis, source, core):
    z, x, y = source
    if piece == 0:
        bit = y + core if axis == "x" else x + y + core
    elif piece == 1:
        bit = y + core if axis == "z" else y + z + core
    else:
        bit = core if axis == "z" else z + core
    return 1 - 2 * (bit % 2)


def gather_schedule(me, core, start, take):
    z, x, y = me

    def moved(axis, step):
        if axis == "z":
            return (z + step + NZ) % NZ, x, y
        if axis == "x":
            return z, (x + step + NX) % NX, y
        return z, x, 1 - y

    def ways(axis):
        return (1,) if axis == "y" else (1, -1)

    for axis in "yzx":
        for piece in OWN_ORDER[axis]:
            for way in ways(axis):
                start(piece, me, moved(axis, way))
    for number, event in enumerate(EVENTS):
        piece, dz, dx, dy, kind = decode(event)
        offset = {"z": dz, "x": dx, "y": dy}
        axis = last_axis(piece, offset)
        source = [(z + dz) % NZ, (x + dx) % NX, (y + dy) % NY]
        onward = None
        if kind:
            way = side(piece, axis, source, core)
            half = LENGTH[axis] // 2
            place = half + way if kind == 1 else half - way
            if axis == "z":
                source[0] = (z + place) % NZ
            else:
                source[1] = (x + place) % NX
            if kind == 1:
                onward = way
        elif axis != "y":
            half = LENGTH[axis] // 2
            if offset[axis] < half - 1:
                onward = -1
            elif offset[axis] > half + 1:
                onward = 1
        take(piece, source)
        if onward is not None:
            start(piece, source, moved(axis, onward))
        for later in AXES[piece][AXES[piece].index(axis) + 1 :]:
            for way in ways(later):
                start(piece, source, moved(later, way))
        yield number


def index_of(place):
    return place[0] * (NX * NY) + place[1] * NY + place[2]


def kernel(
    a_hbm, l_hbm, mask_ref, owner_ref, dinv_ref,
    panel_ref, upper_ref, diag_ref,
    whole, own, other, total, turned, rows_in,
    load_sem, sib_send, sib_recv, send_sem, recv_sem, turn_send, turn_recv,
):
    leaf, here = lax.axis_index("leaf"), lax.axis_index("grid")
    core = leaf % 2
    sibling = leaf + 1 - 2 * core
    me = (here // (NX * NY), here // NY % NX, here % NY)

    mine = pltpu.make_async_copy(
        l_hbm.at[0], whole.at[pl.ds(pl.multiple_of(here * ROWS, ROWS), ROWS)], load_sem.at[0]
    )
    mine.start()
    chunk = SEP // 4
    loads = []
    for part in range(4):
        columns = pl.ds(part * chunk, chunk)
        loads.append(pltpu.make_async_copy(a_hbm.at[0, :, columns], own.at[:, columns], load_sem.at[1 + part]))
        loads[-1].start()

    barrier = pltpu.get_barrier_semaphore()
    pl.semaphore_signal(barrier, inc=1, device_id=(sibling, here), device_id_type=MESH)

    def greet(step, carry):
        pl.semaphore_signal(
            barrier, inc=1, device_id=(leaf, lax.rem(here + step, NGRID)), device_id_type=MESH
        )
        return carry

    lax.fori_loop(1, NGRID, greet, 0)
    pl.semaphore_wait(barrier, NGRID)
    mine.wait()

    sent = []

    def remote(piece, source, place, send):
        block = whole.at[
            pl.ds(pl.multiple_of(index_of(source) * ROWS + FIRST[piece], 16), COUNT[piece])
        ]
        return pltpu.make_async_remote_copy(
            src_ref=block,
            dst_ref=block,
            send_sem=send,
            recv_sem=recv_sem.at[piece, index_of(source)],
            device_id=(leaf, index_of(place)),
            device_id_type=MESH,
        )

    def start(piece, source, place):
        sent.append(remote(piece, source, place, send_sem.at[len(sent)]))
        sent[-1].start()

    def take(piece, source):
        remote(piece, source, me, send_sem.at[0]).wait_recv()

    def multiply(blocks):
        code = sum(block * 32**i for i, block in enumerate(blocks))

        def one(_, code):
            block = code % 32
            number = (me[0] + block // NX) % NZ * NX + (me[1] + block % NX) % NX
            columns = pl.ds(pl.multiple_of(number * B, B), B)
            swap = jnp.full((ROWS, B), owner_ref[number], jnp.int32) == 1
            keep = jnp.full((ROWS, B), mask_ref[number], jnp.int32) == 1
            mixed = jnp.where(swap, other[:, columns], own[:, columns])
            mixed = jnp.where(keep, mixed, jnp.zeros((), jnp.bfloat16))
            total[...] += jnp.dot(mixed, whole[columns, :], preferred_element_type=jnp.float32)
            return code // 32

        lax.fori_loop(0, len(blocks), one, jnp.int32(code))

    swaps = []
    for part in range(4):
        columns = pl.ds(part * chunk, chunk)
        swaps.append(
            pltpu.make_async_remote_copy(
                src_ref=a_hbm.at[0, :, columns],
                dst_ref=other.at[:, columns],
                send_sem=sib_send.at[part],
                recv_sem=sib_recv.at[part],
                device_id=(sibling, here),
                device_id_type=MESH,
            )
        )
    total[...] = jnp.zeros_like(total)
    ready = False
    for number in gather_schedule(me, core, start, take):
        if number == 4:
            for copy in swaps:
                copy.start()
        if number in SITES:
            if not ready:
                for copy in loads:
                    copy.wait()
                for copy in swaps:
                    copy.wait()
                ready = True
            multiply(SITES[number])

    panel = (-total[...]).astype(jnp.bfloat16)
    panel_ref[0] = panel
    turned[...] = panel.astype(jnp.float32).T.reshape(NGRID, B // NGRID, ROWS).astype(jnp.bfloat16)

    def column(place):
        return pl.ds(pl.multiple_of(place * ROWS, ROWS), ROWS)

    def turn(step, back):
        target = lax.rem(here + step, NGRID)
        return pltpu.make_async_remote_copy(
            src_ref=turned.at[target],
            dst_ref=rows_in.at[:, column(here if not back else lax.rem(here - step + NGRID, NGRID))],
            send_sem=turn_send.at[step],
            recv_sem=turn_recv.at[step],
            device_id=(leaf, target),
            device_id_type=MESH,
        )

    def send(step, carry):
        turn(step, False).start()
        return carry

    lax.fori_loop(1, NGRID, send, 0)
    rows_in[:, column(here)] = turned[here]
    for copy in sent:
        copy.wait_send()

    def arrive(step, carry):
        turn(step, True).wait_recv()
        return carry

    lax.fori_loop(1, NGRID, arrive, 0)
    upper_ref[0] = rows_in[...]

    def diagonal(number, total_rows):
        columns = pl.ds(pl.multiple_of(number * B, B), B)
        keep = jnp.full((B // NGRID, B), mask_ref[number], jnp.int32) == 1
        left = jnp.where(keep, rows_in[:, columns], jnp.zeros((), jnp.bfloat16))
        return total_rows + jnp.dot(left, whole[columns, :], preferred_element_type=jnp.float32)

    update = lax.fori_loop(
        0, SEP // B, diagonal, jnp.zeros((B // NGRID, B), jnp.float32), unroll=4
    )
    diag_ref[0] = dinv_ref[0] - update

    def leave(step, carry):
        turn(step, False).wait_send()
        return carry

    lax.fori_loop(1, NGRID, leave, 0)


def body(ainv_sep, l_panel, block_mask, owner, dinv):
    vmem = pl.BlockSpec(memory_space=pltpu.VMEM)
    smem = pl.BlockSpec(memory_space=pltpu.SMEM)
    hbm = pl.BlockSpec(memory_space=pl.ANY)
    dma = pltpu.SemaphoreType.DMA
    return pl.pallas_call(
        kernel,
        out_shape=(
            jax.ShapeDtypeStruct((1, ROWS, B), jnp.bfloat16),
            jax.ShapeDtypeStruct((1, B // NGRID, SEP), jnp.bfloat16),
            jax.ShapeDtypeStruct((1, B // NGRID, B), jnp.float32),
        ),
        in_specs=[hbm, hbm, smem, smem, vmem],
        out_specs=(vmem, vmem, vmem),
        scratch_shapes=[
            pltpu.VMEM((SEP, B), jnp.bfloat16),
            pltpu.VMEM((ROWS, SEP), jnp.bfloat16),
            pltpu.VMEM((ROWS, SEP), jnp.bfloat16),
            pltpu.VMEM((ROWS, B), jnp.float32),
            pltpu.VMEM((NGRID, B // NGRID, ROWS), jnp.bfloat16),
            pltpu.VMEM((B // NGRID, SEP), jnp.bfloat16),
            dma((5,)),
            dma((4,)),
            dma((4,)),
            dma((208,)),
            dma((3, NGRID)),
            dma((NGRID,)),
            dma((NGRID,)),
        ],
        compiler_params=pltpu.CompilerParams(
            collective_id=0, has_side_effects=True, vmem_limit_bytes=60 * 1024 * 1024
        ),
    )(ainv_sep, l_panel, block_mask.reshape(-1), owner.reshape(-1), dinv)


def solution(mesh):
    rows = P("leaf", "grid", None)
    return jax.shard_map(
        body,
        mesh=mesh,
        in_specs=(rows, rows, P("leaf", None, None), P("leaf", None), rows),
        out_specs=(rows, rows, rows),
        check_vma=False,
    )
```

time: 302 us -> 113 us (0.37)
  waiting for transfers between devices: 214 us -> 0 us
  Pallas kernels: 0 us -> 108 us
  blocking collectives: 32.3 us -> 0 us
  matrix products: 24.5 us -> 0 us
  between operations: 14.1 us -> 0.64 us
  local copies, waits for them, and re-layouts: 14.7 us -> 4.66 us
    all_gather x2 -> x0, waiting for transfers between devices: 214 us -> none  [gather_in_order(): tiles = lax.all_gather(tiles, axes[k])]
    pallas_call x0 -> x1, Pallas kernels: none -> 108 us  [body(): pl.pallas_call(kernel, out_shape=(jax.ShapeDtypeStruct((1, ROWS, B), jnp....]
    dot_general x3 -> x0, matrix products: 24.5 us -> none  [the longest x1 15 us: body(): jnp.dot(mixed, whole_panel, preferred_element_type=jnp.float32)]
    all_to_all x1 -> x0, blocking collectives: 23.5 us -> none  [body(): lax.all_to_all(panel.T, GRID, split_axis=0, concat_axis=1, tiled=True)]
    transpose x1 -> x0, local copies, waits for them, and re-layouts: 13.7 us -> none  [gather_in_order(): tiles = tiles.transpose(*back, *range(len(axes), tiles.ndim))]
    all_gather x1 -> x0, blocking collectives: 8.82 us -> none  [gather_in_order(): tiles = lax.all_gather(tiles, axes[k])]
    unnamed x7 -> x3, local copies, waits for them, and re-layouts: 0.81 us -> 4.66 us
  transfers between devices with their start and end apart: 3 -> 0, of which waited for: 2 -> 0; matrix products, arithmetic and copies ran while one was open for 5% -> 0% of each run, Pallas kernels for 0% -> 0%
where the time goes in v1:
time: 113 us
  Pallas kernels  108 us (96%)
  local copies, waits for them, and re-layouts  4.66 us (4%)
    pallas_call x1, Pallas kernels, body(): pl.pallas_call(kernel, out_shape=(jax.ShapeDtypeStruct((1, ROWS, B), jnp....  108 us
    unnamed x3, local copies, waits for them, and re-layouts  4.66 us

profile of v1, /device:TPU:8, one launch (start us, length us, event | category | flops | bytes accessed | tf_op | source)
XLA Modules:
  0.0 113.0 jit_solution(8556727124027274863)
XLA Ops:
  0.6 107.7 %shard_map.76 = (bf16[1,256,512]{2,1,0:T(8,128)(2,1)}, bf16[1,8,16384]{2,1,0:T(8,128)(2,1)}, f32[1,8,512]{2,1,0:T(8,128)}) custom-call(bf16[1,256,16384]{2,1,0:T(8,128)(2,1)} %a_hbm.1, bf16[1,256,512]{2,1,0:T(8,128)(2,1)} %l_hbm.1, s32[32]{0:T(128)} %bitcast.2, s32[32]{0:T(128)} %bitcast.3, f32[1,8,512]{2,1,0:T(8,128)} %dinv_ref.1), custom_call_target="tpu_custom_call" | custom-call | tf_op jit(solution)/shard_map/pallas_call | solution.py:281
  108.4 1.7 %copy.11 = bf16[1,256,512]{2,1,0:T(8,128)(2,1)} copy(bf16[1,256,512]{2,1,0:T(8,128)(2,1)} %get-tuple-element.6) | data formatting | bytes 524288
  110.0 1.7 %copy.12 = bf16[1,8,16384]{2,1,0:T(8,128)(2,1)} copy(bf16[1,8,16384]{2,1,0:T(8,128)(2,1)} %get-tuple-element.7) | data formatting | bytes 524288
  111.7 1.3 %copy.13 = f32[1,8,512]{2,1,0:T(8,128)} copy(f32[1,8,512]{2,1,0:T(8,128)} %get-tuple-element.8) | data formatting | bytes 32768

commit v2 on v1

--- a/solution.py
+++ b/solution.py
@@ -14,6 +14,7 @@
 NZ, NX, NY = 8, 4, 2
 NGRID = NZ * NX * NY
 LENGTH = {"z": NZ, "x": NX, "y": NY}
+WAYS = (("z", 1), ("z", -1), ("x", 1), ("x", -1), ("y", 1))
 
 FIRST = (0, 80, 160)
 COUNT = (80, 80, 96)
@@ -68,15 +69,17 @@
     return 1 - 2 * (bit % 2)
 
 
+def moved(place, axis, step):
+    z, x, y = place
+    if axis == "z":
+        return (z + step + NZ) % NZ, x, y
+    if axis == "x":
+        return z, (x + step + NX) % NX, y
+    return z, x, 1 - y
+
+
 def gather_schedule(me, core, start, take):
     z, x, y = me
-
-    def moved(axis, step):
-        if axis == "z":
-            return (z + step + NZ) % NZ, x, y
-        if axis == "x":
-            return z, (x + step + NX) % NX, y
-        return z, x, 1 - y
 
     def ways(axis):
         return (1,) if axis == "y" else (1, -1)
@@ -84,7 +87,7 @@
     for axis in "yzx":
         for piece in OWN_ORDER[axis]:
             for way in ways(axis):
-                start(piece, me, moved(axis, way))
+                start(piece, me, moved(me, axis, way))
     for number, event in enumerate(EVENTS):
         piece, dz, dx, dy, kind = decode(event)
         offset = {"z": dz, "x": dx, "y": dy}
@@ -109,10 +112,10 @@
                 onward = 1
         take(piece, source)
         if onward is not None:
-            start(piece, source, moved(axis, onward))
+            start(piece, source, moved(me, axis, onward))
         for later in AXES[piece][AXES[piece].index(axis) + 1 :]:
             for way in ways(later):
-                start(piece, source, moved(later, way))
+                start(piece, source, moved(me, later, way))
         yield number
 
 
@@ -144,15 +147,11 @@
 
     barrier = pltpu.get_barrier_semaphore()
     pl.semaphore_signal(barrier, inc=1, device_id=(sibling, here), device_id_type=MESH)
-
-    def greet(step, carry):
+    for axis, way in WAYS:
         pl.semaphore_signal(
-            barrier, inc=1, device_id=(leaf, lax.rem(here + step, NGRID)), device_id_type=MESH
+            barrier, inc=1, device_id=(leaf, index_of(moved(me, axis, way))), device_id_type=MESH
         )
-        return carry
-
-    lax.fori_loop(1, NGRID, greet, 0)
-    pl.semaphore_wait(barrier, NGRID)
+    pl.semaphore_wait(barrier, 1 + len(WAYS))
     mine.wait()
 
     sent = []
@@ -248,22 +247,24 @@
     for copy in sent:
         copy.wait_send()
 
-    def arrive(step, carry):
-        turn(step, True).wait_recv()
-        return carry
-
-    lax.fori_loop(1, NGRID, arrive, 0)
+    def arrive(source):
+        @pl.when(source != here)
+        def _():
+            turn(lax.rem(here - source + NGRID, NGRID), True).wait_recv()
+
+    PLANE = NX * NY
+    update = jnp.zeros((B // NGRID, B), jnp.float32)
+    for dz in (0, 1, 7, 2, 6, 3, 5, 4):
+        plane = (me[0] + dz) % NZ
+        for i in range(PLANE):
+            arrive(plane * PLANE + i)
+        for i in range(PLANE // NY):
+            number = plane * (PLANE // NY) + i
+            columns = pl.ds(pl.multiple_of(number * B, B), B)
+            keep = jnp.full((B // NGRID, B), mask_ref[number], jnp.int32) == 1
+            left = jnp.where(keep, rows_in[:, columns], jnp.zeros((), jnp.bfloat16))
+            update += jnp.dot(left, whole[columns, :], preferred_element_type=jnp.float32)
     upper_ref[0] = rows_in[...]
-
-    def diagonal(number, total_rows):
-        columns = pl.ds(pl.multiple_of(number * B, B), B)
-        keep = jnp.full((B // NGRID, B), mask_ref[number], jnp.int32) == 1
-        left = jnp.where(keep, rows_in[:, columns], jnp.zeros((), jnp.bfloat16))
-        return total_rows + jnp.dot(left, whole[columns, :], preferred_element_type=jnp.float32)
-
-    update = lax.fori_loop(
-        0, SEP // B, diagonal, jnp.zeros((B // NGRID, B), jnp.float32), unroll=4
-    )
     diag_ref[0] = dinv_ref[0] - update
 
     def leave(step, carry):
@@ -281,9 +282,9 @@
     return pl.pallas_call(
         kernel,
         out_shape=(
-            jax.ShapeDtypeStruct((1, ROWS, B), jnp.bfloat16),
-            jax.ShapeDtypeStruct((1, B // NGRID, SEP), jnp.bfloat16),
-            jax.ShapeDtypeStruct((1, B // NGRID, B), jnp.float32),
+            pltpu.VMEM((1, ROWS, B), jnp.bfloat16),
+            pltpu.VMEM((1, B // NGRID, SEP), jnp.bfloat16),
+            pltpu.VMEM((1, B // NGRID, B), jnp.float32),
         ),
         in_specs=[hbm, hbm, smem, smem, vmem],
         out_specs=(vmem, vmem, vmem),

time: 113 us -> 104 us (0.920)
  Pallas kernels: 108 us -> 101 us
  local copies, waits for them, and re-layouts: 4.66 us -> 2.01 us
    pallas_call x1, Pallas kernels: 108 us -> 101 us  [body(): pl.pallas_call(kernel, out_shape=(pltpu.VMEM((1, ROWS, B), jnp.bfloat16),...]
    unnamed x3, local copies, waits for them, and re-layouts: 4.66 us -> 2.01 us
where the time goes in v2:
time: 104 us; the launch traced here: 103 us
  Pallas kernels  101 us (97%)
  local copies, waits for them, and re-layouts  2.01 us (2%)
    pallas_call x1, Pallas kernels, body(): pl.pallas_call(kernel, out_shape=(pltpu.VMEM((1, ROWS, B), jnp.bfloat16),...  101 us

profile of v2, /device:TPU:8, one launch (start us, length us, event | category | flops | bytes accessed | tf_op | source)
XLA Modules:
  0.0 103.4 jit_solution(6933133110249317492)
XLA Ops:
  0.6 100.7 %shard_map.76 = (bf16[1,256,512]{2,1,0:T(8,128)(2,1)S(1)}, bf16[1,8,16384]{2,1,0:T(8,128)(2,1)S(1)}, f32[1,8,512]{2,1,0:T(8,128)S(1)}) custom-call(bf16[1,256,16384]{2,1,0:T(8,128)(2,1)} %a_hbm.1, bf16[1,256,512]{2,1,0:T(8,128)(2,1)} %l_hbm.1, s32[32]{0:T(128)} %bitcast.2, s32[32]{0:T(128)} %bitcast.3, f32[1,8,512]{2,1,0:T(8,128)} %dinv_ref.1), custom_call_target="tpu_custom_call" | custom-call | tf_op jit(solution)/shard_map/pallas_call | solution.py:282
  101.3 0.7 copy.11
  102.0 0.6 copy.13
  102.7 0.7 copy.12

commit v3 on v0

v3 whole, which is shorter than its diff:
```python
import functools

import jax
import jax.numpy as jnp
from jax import lax
from jax.experimental import pallas as pl
from jax.experimental.pallas import tpu as pltpu
from jax.sharding import PartitionSpec as P

MESH = pl.DeviceIdType.MESH
B = 512
SEP = 16384
ROWS = 256
NZ, NX, NY = 8, 4, 2
NGRID = NZ * NX * NY
WAYS = (("z", 1), ("z", -1), ("x", 1), ("x", -1), ("y", 1))

FIRST = (0, 80, 160)
COUNT = (80, 80, 96)
AXES = ("yxz", "yzx", "zxy")
PROGRAM = (
    22000, 32000, 42000, 52000, 12000, 10000, 21000, 31000, 40000, 50000, 11000, 20000, 30000, 41000, 51000,
    92001, 92500, 92100, 92030, 92010, 42100, 2500, 2100, 12100, 42500, 12500, 52500, 12030, 90001, 91500,
    91100, 90030, 90010, 40001, 50001, 1500, 1100, 10, 52100, 20001, 91030, 91010, 90100, 90500, 91001,
    31001, 21001, 12010, 2010, 92110, 92101, 92200, 92600, 2200, 2600, 42200, 20010, 42600, 20030, 92510,
    90031, 90011, 91600, 91200, 20011, 11, 92501, 12200, 41100, 92530, 1200, 20031, 91101, 91501, 1101,
    90020, 41500, 12600, 92031, 92130, 20020, 90101, 52200, 92020, 12510, 92011, 92300, 42300, 1501, 52600,
    92210, 2300, 90111, 90110, 41200, 92700, 90021, 20021, 12110, 92610, 41001, 42700, 90130, 30010, 41101,
    91110, 92201, 12130, 30011, 91300, 91201, 1201, 41300, 91510, 90131, 92310, 30030, 41600, 92601, 12530,
    30031, 90120, 30001, 92230, 2110, 52300, 41501, 30020, 91601, 92511, 92630, 100, 12020, 92400, 91210,
    90121, 42400, 2510, 91301, 92111, 91011, 12300, 92710, 1600, 90510, 91111, 91310, 92131, 90511, 30021,
    101, 2610, 12610, 91610, 90530, 111, 110, 90531, 41201, 90501, 92531, 2210, 12210, 91511, 51300,
    92120, 130, 131, 92330, 90520, 90200, 92021, 12700, 51500, 52700, 120, 41601, 92410, 92520, 500,
    1601, 91700, 51100, 92301, 12630, 41700, 2310, 1301, 121, 90521, 90201, 501, 92620, 92611, 12230,
    90211, 90210, 1010, 91211, 92220, 511, 530, 92211, 91330, 12120, 2710, 90230, 90231, 51001, 531,
    510, 51200, 91530, 92701, 91611, 92730, 90220, 12520, 52400, 51101, 520, 90600, 200, 91701, 91130,
    91710, 92631, 41301, 12310, 91401, 201, 51600, 92320, 90221, 521, 90601, 41701, 210, 92231, 51501,
    12710, 91020, 90611, 90630, 211, 230, 51201, 1510, 61310, 92121, 91031, 92720, 12400, 91230, 90631,
    90610, 231, 2410, 1110, 600, 92430, 92521, 12330, 90620, 91131, 220, 51601, 90300, 221, 91311,
    90301, 91630, 1210, 92311, 90621, 12620, 1011, 1300, 91711, 630, 90310, 91531, 1111, 41401, 92711,
    12220, 611, 90311, 610, 90330, 91231, 91410, 1610, 91520, 1310, 92401, 12730, 90331, 631, 601,
    1511, 92420, 91120, 51301, 90700, 90320, 91631, 620, 92331, 12410, 300, 51700, 1211, 90321, 61330,
    91220, 91021, 92621, 621, 12320, 91400, 51401, 1611, 90730, 301, 91121, 91411, 311, 92221, 1311,
    90711, 12720, 51701, 90710, 310, 91620, 91320, 331, 1410, 90701, 90731, 1710, 92731, 12430, 330,
    91521, 320, 91331, 1711, 1411, 90720, 321, 90400, 12420, 92411, 91730, 91221, 91430, 90721, 91431,
    92321, 91621, 90401, 90411, 91321, 91731, 92721, 90410, 90431, 91420, 91720, 90430, 92431, 90420, 91721,
    91421, 90421, 92421,
)
SITES = {
    159: (0, 4,),
    235: (28, 8,),
    250: (24, 1,),
    281: (3, 5,),
    290: (7, 29,),
    306: (31, 9,),
    315: (11, 25,),
    325: (27, 2,),
    339: (12, 20,),
    345: (6, 30,),
    361: (10, 26,),
    365: (16, 13,),
    369: (15, 21,),
    374: (23, 17,),
    377: (19, 14, 22, 18,),
}


def decode(item):
    return item // 10000, item // 1000 % 10, item // 100 % 10, item // 10 % 10, item % 10


def wrap(value, length):
    return value % length if isinstance(value, int) else lax.rem(value, length)


def side(piece, axis, source, core):
    z, x, y = source
    if piece == 0:
        bit = y + core if axis == "x" else x + y + core
    elif piece == 1:
        bit = y + core if axis == "z" else y + z + core
    else:
        bit = core if axis == "z" else z + core
    return 1 - 2 * wrap(bit, 2)


def locate(piece, kz, kx, dy, me, core):
    source = list(me)
    for axis in AXES[piece]:
        if axis == "y" and dy:
            source[2] = 1 - me[2]
        elif axis == "z" and kz:
            way = side(piece, axis, source, core)
            source[0] = wrap(me[0] + NZ + (-way * kz if kz <= 4 else way * (kz - 4)), NZ)
        elif axis == "x" and kx:
            way = side(piece, axis, source, core)
            source[1] = wrap(me[1] + NX + (-way * kx if kx <= 2 else way), NX)
    return tuple(source)


def moved(place, axis, step):
    z, x, y = place
    if axis == "z":
        return wrap(z + step + NZ, NZ), x, y
    if axis == "x":
        return z, wrap(x + step + NX, NX), y
    return z, x, 1 - y


def gather_schedule(me, core, start, take):
    for number, item in enumerate(PROGRAM):
        what, piece, kz, kx, dy = decode(item)
        source = locate(piece, kz, kx, dy, me, core)
        if what == 9:
            take(piece, source)
        else:
            short = what in (3, 5)
            if what:
                axis = {1: "y", 2: "z", 3: "z", 4: "x", 5: "x", 6: "z"}[what]
            else:
                places = {"z": kz, "x": kx, "y": dy}
                axis = [axis for axis in AXES[piece] if places[axis]][-1]
                short = axis == "z" and kz > 4
            way = side(piece, axis, source, core) if axis != "y" else 1
            start(piece, source, moved(me, axis, -way if short else way))
        yield number


def index_of(place):
    return place[0] * PLANE + place[1] * NY + place[2]


PLANE = NX * NY
SENT = 63
CHUNK = 1024
MIX_FROM = 110
MIX_STEP = 3


def kernel(
    a_hbm, l_hbm, mask_hbm, owner_hbm, dinv_hbm,
    panel_ref, upper_ref, diag_ref,
    whole, own, other, total, turned, mask_ref, owner_ref, dinv_ref,
    load_sem, send_sem, recv_sem, turn_send, turn_recv,
):
    leaf, here = lax.axis_index("leaf"), lax.axis_index("grid")
    core = lax.rem(leaf, 2)
    sibling = leaf + 1 - 2 * core
    me = (here // PLANE, lax.rem(here // NY, NX), lax.rem(here, NY))

    mine = pltpu.make_async_copy(
        l_hbm.at[0], whole.at[pl.ds(pl.multiple_of(here * ROWS, ROWS), ROWS)], load_sem.at[0]
    )
    mine.start()

    barrier = pltpu.get_barrier_semaphore()
    pl.semaphore_signal(barrier, inc=1, device_id=(sibling, here), device_id_type=MESH)
    for axis, way in WAYS:
        pl.semaphore_signal(
            barrier, inc=1, device_id=(leaf, index_of(moved(me, axis, way))), device_id_type=MESH
        )
    small = [
        pltpu.make_async_copy(mask_hbm, mask_ref, load_sem.at[1]),
        pltpu.make_async_copy(owner_hbm, owner_ref, load_sem.at[2]),
        pltpu.make_async_copy(dinv_hbm.at[0], dinv_ref, load_sem.at[3]),
    ]
    for copy in small:
        copy.start()
    pl.semaphore_wait(barrier, 1 + len(WAYS))
    mine.wait()

    def remote(piece, source, place):
        block = whole.at[
            pl.ds(pl.multiple_of(index_of(source) * ROWS + FIRST[piece], 16), COUNT[piece])
        ]
        return pltpu.make_async_remote_copy(
            src_ref=block,
            dst_ref=block,
            send_sem=send_sem.at[piece],
            recv_sem=recv_sem.at[piece, index_of(source)],
            device_id=(leaf, index_of(place)),
            device_id_type=MESH,
        )

    def start(piece, source, place):
        remote(piece, source, place).start()

    def take(piece, source):
        remote(piece, source, me).wait_recv()

    def multiply(blocks):
        product = None
        for block in blocks:
            number = moved(me, "z", block // NX)[0] * NX + moved(me, "x", block % NX)[1]
            columns = pl.ds(pl.multiple_of(number * B, B), B)
            part = jnp.dot(own[:, columns], whole[columns, :], preferred_element_type=jnp.float32)
            product = part if product is None else product + part
        total[...] += product

    def mix(first, count):
        def one(number, carry):
            columns = pl.ds(pl.multiple_of(number * B, B), B)
            swap = jnp.full((ROWS, B), owner_ref[number], jnp.int32) == 1
            keep = jnp.full((ROWS, B), mask_ref[number], jnp.int32) == 1
            mixed = jnp.where(swap, other[:, columns], own[:, columns])
            own[:, columns] = jnp.where(keep, mixed, jnp.zeros((), jnp.bfloat16))
            return carry

        lax.fori_loop(first, first + count, one, 0)

    def load(columns):
        return pltpu.make_async_copy(a_hbm.at[0, :, columns], own.at[:, columns], load_sem.at[4])

    def swap(columns):
        return pltpu.make_async_remote_copy(
            src_ref=a_hbm.at[0, :, columns],
            dst_ref=other.at[:, columns],
            send_sem=load_sem.at[5],
            recv_sem=load_sem.at[6],
            device_id=(sibling, here),
            device_id_type=MESH,
        )

    total[...] = jnp.zeros_like(total)
    issued, mixed = 0, 0
    for number in gather_schedule(me, core, start, take):
        if number % 4 == 3 and issued < SEP // CHUNK:
            columns = pl.ds(issued * CHUNK, CHUNK)
            load(columns).start()
            swap(columns).start()
            issued += 1
        if number == MIX_FROM:
            everything = pl.ds(0, SEP)
            for copy in small[:2] + [load(everything), swap(everything)]:
                copy.wait()
        if number >= MIX_FROM and (number - MIX_FROM) % MIX_STEP == 0 and mixed < SEP // B:
            mix(mixed, 2)
            mixed += 2
        if number in SITES:
            multiply(SITES[number])

    panel = (-total[...]).astype(jnp.bfloat16)
    turned[...] = panel.astype(jnp.float32).T.reshape(NGRID, B // NGRID, ROWS).astype(jnp.bfloat16)
    panel_ref[0] = panel

    rows_in = upper_ref.at[0]

    def column(place):
        return pl.ds(pl.multiple_of(place * ROWS, ROWS), ROWS)

    def turn(block, source, target):
        return pltpu.make_async_remote_copy(
            src_ref=block,
            dst_ref=rows_in.at[:, column(source)],
            send_sem=turn_send.at[0],
            recv_sem=turn_recv.at[source // PLANE],
            device_id=(leaf, target),
            device_id_type=MESH,
        )

    for dz in (4, 3, 5, 2, 6, 1, 7, 0):
        plane = moved(me, "z", dz)[0] * PLANE
        for i in range(PLANE):
            if dz == 0 and i == 0:
                continue
            target = plane + (here + i) % PLANE
            turn(turned.at[target], here, target).start()
    rows_in[:, column(here)] = turned[here]
    for piece in range(3):
        rows = whole.at[pl.ds(0, SENT * COUNT[piece])]
        pltpu.make_async_remote_copy(
            src_ref=rows, dst_ref=rows, send_sem=send_sem.at[piece], recv_sem=recv_sem.at[piece, 0],
            device_id=(sibling, here), device_id_type=MESH,
        ).wait_send()

    update = jnp.zeros((B // NGRID, B), jnp.float32)
    for dz in (0, 7, 1, 6, 2, 5, 3, 4):
        plane = moved(me, "z", dz)[0]
        count = PLANE if dz else PLANE - 1
        arrived = rows_in.at[:, pl.ds(0, count * ROWS)]
        pltpu.make_async_remote_copy(
            src_ref=arrived, dst_ref=arrived, send_sem=turn_send.at[0], recv_sem=turn_recv.at[plane],
            device_id=(sibling, here), device_id_type=MESH,
        ).wait_recv()
        for i in range(PLANE // NY):
            number = plane * (PLANE // NY) + i
            columns = pl.ds(pl.multiple_of(number * B, B), B)
            keep = jnp.full((B // NGRID, B), mask_ref[number], jnp.int32) == 1
            left = jnp.where(keep, rows_in[:, columns], jnp.zeros((), jnp.bfloat16))
            update += jnp.dot(left, whole[columns, :], preferred_element_type=jnp.float32)
    small[2].wait()
    diag_ref[0] = dinv_ref[...] - update

    direct = turned.at[pl.ds(0, NGRID - 1)]
    pltpu.make_async_remote_copy(
        src_ref=direct, dst_ref=direct, send_sem=turn_send.at[0], recv_sem=turn_recv.at[0],
        device_id=(sibling, here), device_id_type=MESH,
    ).wait_send()


def put_out(panel_ref, upper_ref, diag_ref, panel_out, upper_out, diag_out, sem):
    pairs = ((panel_ref, panel_out), (upper_ref, upper_out), (diag_ref, diag_out))
    copies = [pltpu.make_async_copy(a, b, sem.at[i]) for i, (a, b) in enumerate(pairs)]
    for copy in copies:
        copy.start()
    for copy in copies:
        copy.wait()


def body(ainv_sep, l_panel, block_mask, owner, dinv):
    vmem = pl.BlockSpec(memory_space=pltpu.VMEM)
    hbm = pl.BlockSpec(memory_space=pl.ANY)
    dma = pltpu.SemaphoreType.DMA
    shapes = (
        ((1, ROWS, B), jnp.bfloat16),
        ((1, B // NGRID, SEP), jnp.bfloat16),
        ((1, B // NGRID, B), jnp.float32),
    )
    results = pl.pallas_call(
        kernel,
        out_shape=tuple(pltpu.VMEM(*shape) for shape in shapes),
        in_specs=[hbm] * 5,
        out_specs=(vmem, vmem, vmem),
        scratch_shapes=[
            pltpu.VMEM((SEP, B), jnp.bfloat16),
            pltpu.VMEM((ROWS, SEP), jnp.bfloat16),
            pltpu.VMEM((ROWS, SEP), jnp.bfloat16),
            pltpu.VMEM((ROWS, B), jnp.float32),
            pltpu.VMEM((NGRID, B // NGRID, ROWS), jnp.bfloat16),
            pltpu.SMEM((SEP // B,), jnp.int32),
            pltpu.SMEM((SEP // B,), jnp.int32),
            pltpu.VMEM((B // NGRID, B), jnp.float32),
            dma((7,)),
            dma((3,)),
            dma((3, NGRID)),
            dma((1,)),
            dma((NZ,)),
        ],
        compiler_params=pltpu.CompilerParams(
            collective_id=0, has_side_effects=True, vmem_limit_bytes=60 * 1024 * 1024
        ),
    )(ainv_sep, l_panel, block_mask.reshape(-1), owner.reshape(-1), dinv)
    results = [pltpu.with_memory_space_constraint(result, pltpu.VMEM) for result in results]
    return pl.pallas_call(
        put_out,
        out_shape=tuple(jax.ShapeDtypeStruct(*shape) for shape in shapes),
        in_specs=[vmem] * 3,
        out_specs=(hbm, hbm, hbm),
        scratch_shapes=[dma((3,))],
    )(*results)


def solution(mesh):
    rows = P("leaf", "grid", None)
    return jax.shard_map(
        body,
        mesh=mesh,
        in_specs=(rows, rows, P("leaf", None, None), P("leaf", None), rows),
        out_specs=(rows, rows, rows),
        check_vma=False,
    )
```

time: 302 us -> 96.4 us (0.32)
  waiting for transfers between devices: 214 us -> 0 us
  Pallas kernels: 0 us -> 94.7 us
  blocking collectives: 32.3 us -> 0 us
  matrix products: 24.5 us -> 0 us
  local copies, waits for them, and re-layouts: 14.7 us -> 0 us
  between operations: 14.1 us -> 0.64 us
    all_gather x2 -> x0, waiting for transfers between devices: 214 us -> none  [gather_in_order(): tiles = lax.all_gather(tiles, axes[k])]
    pallas_call x0 -> x2, Pallas kernels: none -> 94.7 us  [the longest x1 93.9 us: body(): pl.pallas_call(kernel, out_shape=tuple((pltpu.VMEM(*shape) for shape in s...]
    dot_general x3 -> x0, matrix products: 24.5 us -> none  [the longest x1 15 us: body(): jnp.dot(mixed, whole_panel, preferred_element_type=jnp.float32)]
    all_to_all x1 -> x0, blocking collectives: 23.5 us -> none  [body(): lax.all_to_all(panel.T, GRID, split_axis=0, concat_axis=1, tiled=True)]
    transpose x1 -> x0, local copies, waits for them, and re-layouts: 13.7 us -> none  [gather_in_order(): tiles = tiles.transpose(*back, *range(len(axes), tiles.ndim))]
    all_gather x1 -> x0, blocking collectives: 8.82 us -> none  [gather_in_order(): tiles = lax.all_gather(tiles, axes[k])]
  transfers between devices with their start and end apart: 3 -> 0, of which waited for: 2 -> 0; matrix products, arithmetic and copies ran while one was open for 5% -> 0% of each run, Pallas kernels for 0% -> 0%
where the time goes in v3:
time: 96.4 us; the launch traced here: 95.3 us
  Pallas kernels  94.7 us (98%)
    pallas_call x1, Pallas kernels, body(): pl.pallas_call(kernel, out_shape=tuple((pltpu.VMEM(*shape) for shape in s...  93.9 us

profile of v3, /device:TPU:8, one launch (start us, length us, event | category | flops | bytes accessed | tf_op | source)
XLA Modules:
  0.0 95.3 jit_solution(5017006804759894088)
XLA Ops:
  0.6 93.9 %shard_map.76 = (bf16[1,256,512]{2,1,0:T(8,128)(2,1)S(1)}, bf16[1,8,16384]{2,1,0:T(8,128)(2,1)S(1)}, f32[1,8,512]{2,1,0:T(8,128)S(1)}) custom-call(bf16[1,256,16384]{2,1,0:T(8,128)(2,1)} %a_hbm.1, bf16[1,256,512]{2,1,0:T(8,128)(2,1)} %l_hbm.1, s32[32]{0:T(128)} %bitcast.2, s32[32]{0:T(128)} %bitcast.3, f32[1,8,512]{2,1,0:T(8,128)} %dinv_hbm.1), custom_call_target="tpu_custom_call" | custom-call | tf_op jit(solution)/shard_map/pallas_call | solution.py:319
  94.5 0.8 shard_map.77

commit v4 on v3

--- a/solution.py
+++ b/solution.py
@@ -48,20 +48,16 @@
 )
 SITES = {
     159: (0, 4,),
-    235: (28, 8,),
-    250: (24, 1,),
-    281: (3, 5,),
-    290: (7, 29,),
-    306: (31, 9,),
-    315: (11, 25,),
-    325: (27, 2,),
-    339: (12, 20,),
-    345: (6, 30,),
+    235: (28, 24,),
+    250: (8, 1,),
+    290: (3, 29, 5, 7,),
+    316: (31, 2, 27, 11, 25, 9,),
+    342: (20, 12,),
+    352: (30, 6,),
     361: (10, 26,),
-    365: (16, 13,),
-    369: (15, 21,),
-    374: (23, 17,),
-    377: (19, 14, 22, 18,),
+    365: (21, 16, 13, 23,),
+    373: (15, 19,),
+    377: (17, 22, 14, 18,),
 }
 
 
@@ -110,10 +106,11 @@
 def gather_schedule(me, core, start, take):
     for number, item in enumerate(PROGRAM):
         what, piece, kz, kx, dy = decode(item)
-        source = locate(piece, kz, kx, dy, me, core)
         if what == 9:
-            take(piece, source)
+            if number in ENDS:
+                take(ENDS[number])
         else:
+            source = locate(piece, kz, kx, dy, me, core)
             short = what in (3, 5)
             if what:
                 axis = {1: "y", 2: "z", 3: "z", 4: "x", 5: "x", 6: "z"}[what]
@@ -122,8 +119,51 @@
                 axis = [axis for axis in AXES[piece] if places[axis]][-1]
                 short = axis == "z" and kz > 4
             way = side(piece, axis, source, core) if axis != "y" else 1
-            start(piece, source, moved(me, axis, -way if short else way))
+            start(piece, source, moved(me, axis, -way if short else way), SLOTS[receiver(what, piece, kz, kx, dy)])
         yield number
+
+
+def receiver(what, piece, kz, kx, dy):
+    if what == 0:
+        if [axis for axis in AXES[piece] if {"z": kz, "x": kx, "y": dy}[axis]][-1] == "z":
+            return piece, kz + 1, kx, dy
+        return piece, kz, kx + 1, dy
+    if what == 1:
+        return piece, kz, kx, 1
+    if what in (2, 3):
+        return piece, 1 if what == 2 else 5, kx, dy
+    if what in (4, 5):
+        return piece, kz, 1 if what == 4 else 3, dy
+    return piece, 4, kx, dy
+
+
+def receive_slots(together):
+    keys = {decode(item)[1:] for item in PROGRAM if item // 10000 != 9}
+    slots, ends, last = {}, {}, []
+    count = 0
+    for number, item in enumerate(PROGRAM):
+        what, *key = decode(item)
+        key = tuple(key)
+        if what != 9:
+            continue
+        if key in keys:
+            slots[key] = count
+            ends[number] = [key]
+            count += 1
+            continue
+        last.append((number, key))
+        if len(last) == together:
+            ends[number] = [key for _, key in last]
+            for _, key in last:
+                slots[key] = count
+            count += 1
+            last = []
+    if last:
+        ends[last[-1][0]] = [key for _, key in last]
+        for _, key in last:
+            slots[key] = count
+        count += 1
+    return slots, ends, count
 
 
 def index_of(place):
@@ -133,6 +173,8 @@
 PLANE = NX * NY
 SENT = 63
 CHUNK = 1024
+TOGETHER = 4
+SLOTS, ENDS, SLOT_COUNT = receive_slots(TOGETHER)
 MIX_FROM = 110
 MIX_STEP = 3
 
@@ -169,24 +211,25 @@
     pl.semaphore_wait(barrier, 1 + len(WAYS))
     mine.wait()
 
-    def remote(piece, source, place):
+    def start(piece, source, place, slot):
         block = whole.at[
             pl.ds(pl.multiple_of(index_of(source) * ROWS + FIRST[piece], 16), COUNT[piece])
         ]
-        return pltpu.make_async_remote_copy(
+        pltpu.make_async_remote_copy(
             src_ref=block,
             dst_ref=block,
             send_sem=send_sem.at[piece],
-            recv_sem=recv_sem.at[piece, index_of(source)],
+            recv_sem=recv_sem.at[slot],
             device_id=(leaf, index_of(place)),
             device_id_type=MESH,
-        )
-
-    def start(piece, source, place):
-        remote(piece, source, place).start()
-
-    def take(piece, source):
-        remote(piece, source, me).wait_recv()
+        ).start()
+
+    def take(places):
+        rows = whole.at[pl.ds(0, sum(COUNT[place[0]] for place in places))]
+        pltpu.make_async_remote_copy(
+            src_ref=rows, dst_ref=rows, send_sem=send_sem.at[0], recv_sem=recv_sem.at[SLOTS[places[0]]],
+            device_id=(sibling, here), device_id_type=MESH,
+        ).wait_recv()
 
     def multiply(blocks):
         product = None
@@ -258,7 +301,7 @@
             device_id_type=MESH,
         )
 
-    for dz in (4, 3, 5, 2, 6, 1, 7, 0):
+    for dz in (4, 3, 5, 1, 7, 2, 6, 0):
         plane = moved(me, "z", dz)[0] * PLANE
         for i in range(PLANE):
             if dz == 0 and i == 0:
@@ -269,12 +312,12 @@
     for piece in range(3):
         rows = whole.at[pl.ds(0, SENT * COUNT[piece])]
         pltpu.make_async_remote_copy(
-            src_ref=rows, dst_ref=rows, send_sem=send_sem.at[piece], recv_sem=recv_sem.at[piece, 0],
+            src_ref=rows, dst_ref=rows, send_sem=send_sem.at[piece], recv_sem=recv_sem.at[0],
             device_id=(sibling, here), device_id_type=MESH,
         ).wait_send()
 
     update = jnp.zeros((B // NGRID, B), jnp.float32)
-    for dz in (0, 7, 1, 6, 2, 5, 3, 4):
+    for dz in (4, 0, 3, 5, 1, 7, 6, 2):
         plane = moved(me, "z", dz)[0]
         count = PLANE if dz else PLANE - 1
         arrived = rows_in.at[:, pl.ds(0, count * ROWS)]
@@ -332,7 +375,7 @@
             pltpu.VMEM((B // NGRID, B), jnp.float32),
             dma((7,)),
             dma((3,)),
-            dma((3, NGRID)),
+            dma((SLOT_COUNT,)),
             dma((1,)),
             dma((NZ,)),
         ],

time: 96.4 us -> 94 us (0.975)
  Pallas kernels: 94.7 us -> 92.6 us
    pallas_call x1, Pallas kernels: 93.9 us -> 91.8 us  [body(): pl.pallas_call(kernel, out_shape=tuple((pltpu.VMEM(*shape) for shape in s...]
where the time goes in v4:
time: 94 us; the launch traced here: 93.2 us
  Pallas kernels  92.6 us (99%)
    pallas_call x1, Pallas kernels, body(): pl.pallas_call(kernel, out_shape=tuple((pltpu.VMEM(*shape) for shape in s...  91.8 us

profile of v4, /device:TPU:8, one launch (start us, length us, event | category | flops | bytes accessed | tf_op | source)
XLA Modules:
  0.0 93.2 jit_solution(17477991004009814203)
XLA Ops:
  0.6 91.8 %shard_map.76 = (bf16[1,256,512]{2,1,0:T(8,128)(2,1)S(1)}, bf16[1,8,16384]{2,1,0:T(8,128)(2,1)S(1)}, f32[1,8,512]{2,1,0:T(8,128)S(1)}) custom-call(bf16[1,256,16384]{2,1,0:T(8,128)(2,1)} %a_hbm.1, bf16[1,256,512]{2,1,0:T(8,128)(2,1)} %l_hbm.1, s32[32]{0:T(128)} %bitcast.2, s32[32]{0:T(128)} %bitcast.3, f32[1,8,512]{2,1,0:T(8,128)} %dinv_hbm.1), custom_call_target="tpu_custom_call" | custom-call | tf_op jit(solution)/shard_map/pallas_call | solution.py:362
  92.4 0.8 shard_map.77

commit v5 on v4

--- a/solution.py
+++ b/solution.py
@@ -19,45 +19,45 @@
 COUNT = (80, 80, 96)
 AXES = ("yxz", "yzx", "zxy")
 PROGRAM = (
-    22000, 32000, 42000, 52000, 12000, 10000, 21000, 31000, 40000, 50000, 11000, 20000, 30000, 41000, 51000,
-    92001, 92500, 92100, 92030, 92010, 42100, 2500, 2100, 12100, 42500, 12500, 52500, 12030, 90001, 91500,
-    91100, 90030, 90010, 40001, 50001, 1500, 1100, 10, 52100, 20001, 91030, 91010, 90100, 90500, 91001,
-    31001, 21001, 12010, 2010, 92110, 92101, 92200, 92600, 2200, 2600, 42200, 20010, 42600, 20030, 92510,
-    90031, 90011, 91600, 91200, 20011, 11, 92501, 12200, 41100, 92530, 1200, 20031, 91101, 91501, 1101,
-    90020, 41500, 12600, 92031, 92130, 20020, 90101, 52200, 92020, 12510, 92011, 92300, 42300, 1501, 52600,
-    92210, 2300, 90111, 90110, 41200, 92700, 90021, 20021, 12110, 92610, 41001, 42700, 90130, 30010, 41101,
-    91110, 92201, 12130, 30011, 91300, 91201, 1201, 41300, 91510, 90131, 92310, 30030, 41600, 92601, 12530,
-    30031, 90120, 30001, 92230, 2110, 52300, 41501, 30020, 91601, 92511, 92630, 100, 12020, 92400, 91210,
-    90121, 42400, 2510, 91301, 92111, 91011, 12300, 92710, 1600, 90510, 91111, 91310, 92131, 90511, 30021,
-    101, 2610, 12610, 91610, 90530, 111, 110, 90531, 41201, 90501, 92531, 2210, 12210, 91511, 51300,
-    92120, 130, 131, 92330, 90520, 90200, 92021, 12700, 51500, 52700, 120, 41601, 92410, 92520, 500,
-    1601, 91700, 51100, 92301, 12630, 41700, 2310, 1301, 121, 90521, 90201, 501, 92620, 92611, 12230,
-    90211, 90210, 1010, 91211, 92220, 511, 530, 92211, 91330, 12120, 2710, 90230, 90231, 51001, 531,
-    510, 51200, 91530, 92701, 91611, 92730, 90220, 12520, 52400, 51101, 520, 90600, 200, 91701, 91130,
-    91710, 92631, 41301, 12310, 91401, 201, 51600, 92320, 90221, 521, 90601, 41701, 210, 92231, 51501,
-    12710, 91020, 90611, 90630, 211, 230, 51201, 1510, 61310, 92121, 91031, 92720, 12400, 91230, 90631,
-    90610, 231, 2410, 1110, 600, 92430, 92521, 12330, 90620, 91131, 220, 51601, 90300, 221, 91311,
-    90301, 91630, 1210, 92311, 90621, 12620, 1011, 1300, 91711, 630, 90310, 91531, 1111, 41401, 92711,
-    12220, 611, 90311, 610, 90330, 91231, 91410, 1610, 91520, 1310, 92401, 12730, 90331, 631, 601,
-    1511, 92420, 91120, 51301, 90700, 90320, 91631, 620, 92331, 12410, 300, 51700, 1211, 90321, 61330,
-    91220, 91021, 92621, 621, 12320, 91400, 51401, 1611, 90730, 301, 91121, 91411, 311, 92221, 1311,
-    90711, 12720, 51701, 90710, 310, 91620, 91320, 331, 1410, 90701, 90731, 1710, 92731, 12430, 330,
-    91521, 320, 91331, 1711, 1411, 90720, 321, 90400, 12420, 92411, 91730, 91221, 91430, 90721, 91431,
-    92321, 91621, 90401, 90411, 91321, 91731, 92721, 90410, 90431, 91420, 91720, 90430, 92431, 90420, 91721,
-    91421, 90421, 92421,
+    22000, 32000, 42000, 52000, 12000, 10000, 21000, 31000, 50000, 40000, 11000, 20000, 30000, 41000, 51000,
+    92001, 92500, 92100, 92030, 92010, 2500, 2100, 42100, 12100, 52500, 52100, 12500, 42500, 12030, 2010,
+    12010, 90001, 91500, 91100, 90010, 90030, 1100, 20001, 1500, 20010, 50001, 40001, 20030, 10, 91001,
+    90500, 90100, 91030, 91010, 31001, 21001, 92200, 92600, 52600, 2200, 2600, 12200, 42200, 52200, 12600,
+    42600, 92530, 92101, 92110, 2110, 91200, 92501, 92130, 92510, 12510, 2510, 12110, 90101, 30010, 41100,
+    1200, 91600, 92020, 92031, 90110, 12130, 30030, 90031, 20031, 90011, 20011, 11, 41500, 91501, 91101,
+    1101, 90130, 30011, 30001, 92011, 12530, 90020, 20020, 92630, 92700, 42700, 92300, 42300, 52300, 2300,
+    30031, 92201, 1501, 90111, 12020, 41001, 92210, 92230, 2210, 30020, 41200, 100, 92601, 12300, 90021,
+    20021, 92610, 2610, 101, 91201, 41101, 52700, 90131, 92120, 92511, 41501, 130, 12610, 90120, 30021,
+    1201, 92520, 41600, 110, 92111, 90510, 12210, 111, 91110, 90121, 91300, 41300, 92310, 92330, 90530,
+    2310, 92131, 91510, 1600, 92400, 12700, 51100, 42400, 131, 90511, 90501, 41201, 500, 92531, 51500,
+    12630, 92710, 120, 92620, 90531, 2710, 121, 91601, 91011, 92021, 530, 12230, 90520, 91210, 92220,
+    90200, 41601, 501, 1010, 91111, 511, 92301, 90201, 12120, 92730, 52400, 1601, 51200, 510, 51001,
+    91511, 531, 90230, 92611, 90521, 91301, 51101, 12520, 91310, 91610, 520, 90210, 200, 90211, 92211,
+    51300, 12310, 201, 521, 91700, 41700, 51501, 92320, 41301, 91130, 92701, 92410, 90231, 12710, 230,
+    91211, 90600, 2410, 51600, 91530, 90220, 211, 92631, 1301, 210, 12400, 90221, 51201, 92720, 90630,
+    231, 1110, 92231, 91611, 12330, 600, 90601, 91020, 220, 90611, 1510, 51601, 91701, 41701, 91230,
+    92121, 92430, 12620, 221, 90610, 91031, 601, 90631, 1011, 1210, 91131, 92521, 12220, 630, 90620,
+    611, 1310, 90300, 1111, 91710, 91330, 61310, 92311, 610, 90301, 12730, 51301, 90621, 1511, 91531,
+    91311, 631, 90330, 92711, 1300, 12410, 1610, 91630, 92420, 620, 90311, 91401, 41401, 300, 90310,
+    91231, 1211, 92401, 51700, 12320, 301, 90331, 621, 91120, 91711, 51701, 1311, 92331, 90700, 12720,
+    330, 90320, 311, 91520, 91631, 1611, 51401, 90321, 92621, 310, 90701, 12430, 91021, 91220, 331,
+    1710, 1711, 90730, 61330, 92221, 321, 320, 90711, 12420, 91320, 91121, 91410, 1410, 90710, 91331,
+    92731, 91521, 90731, 91400, 91411, 1411, 91620, 92411, 90720, 90400, 91221, 91730, 92321, 90401, 90721,
+    91731, 91321, 90430, 90411, 92721, 91621, 91431, 90410, 90431, 92431, 91720, 91721, 91430, 90421, 90420,
+    91421, 91420, 92421,
 )
 SITES = {
-    159: (0, 4,),
-    235: (28, 24,),
-    250: (8, 1,),
-    290: (3, 29, 5, 7,),
-    316: (31, 2, 27, 11, 25, 9,),
-    342: (20, 12,),
-    352: (30, 6,),
-    361: (10, 26,),
-    365: (21, 16, 13, 23,),
-    373: (15, 19,),
-    377: (17, 22, 14, 18,),
+    160: (0, 4,),
+    246: (28, 24,),
+    277: (8, 1,),
+    300: (3, 7, 29, 31,),
+    325: (5, 9, 12, 20, 27, 25,),
+    334: (11, 2,),
+    347: (30, 6,),
+    361: (21, 23, 16, 13,),
+    365: (15, 10,),
+    373: (26, 22, 19, 14,),
+    377: (17, 18,),
 }
 
 
@@ -173,6 +173,7 @@
 PLANE = NX * NY
 SENT = 63
 CHUNK = 1024
+TURN_ORDER = (0, 1, 2, 3, 7, 5, 6, 4)
 TOGETHER = 4
 SLOTS, ENDS, SLOT_COUNT = receive_slots(TOGETHER)
 MIX_FROM = 110
@@ -301,13 +302,14 @@
             device_id_type=MESH,
         )
 
-    for dz in (4, 3, 5, 1, 7, 2, 6, 0):
-        plane = moved(me, "z", dz)[0] * PLANE
+    for plane in TURN_ORDER:
         for i in range(PLANE):
-            if dz == 0 and i == 0:
-                continue
-            target = plane + (here + i) % PLANE
-            turn(turned.at[target], here, target).start()
+            target = plane * PLANE + lax.rem(here + i, PLANE)
+            send = turn(turned.at[target], here, target)
+            if i:
+                send.start()
+            else:
+                pl.when(plane != me[0])(send.start)
     rows_in[:, column(here)] = turned[here]
     for piece in range(3):
         rows = whole.at[pl.ds(0, SENT * COUNT[piece])]
@@ -317,7 +319,7 @@
         ).wait_send()
 
     update = jnp.zeros((B // NGRID, B), jnp.float32)
-    for dz in (4, 0, 3, 5, 1, 7, 6, 2):
+    for dz in (0, 1, 7, 2, 6, 3, 5, 4):
         plane = moved(me, "z", dz)[0]
         count = PLANE if dz else PLANE - 1
         arrived = rows_in.at[:, pl.ds(0, count * ROWS)]

time: 94 us -> 92.5 us (0.984)
  Pallas kernels: 92.6 us -> 91.1 us
    pallas_call x1, Pallas kernels: 91.8 us -> 90.3 us  [body(): pl.pallas_call(kernel, out_shape=tuple((pltpu.VMEM(*shape) for shape in s...]
where the time goes in v5:
time: 92.5 us; the launch traced here: 91.7 us
  Pallas kernels  91.1 us (98%)
    pallas_call x1, Pallas kernels, body(): pl.pallas_call(kernel, out_shape=tuple((pltpu.VMEM(*shape) for shape in s...  90.3 us

profile of v5, /device:TPU:8, one launch (start us, length us, event | category | flops | bytes accessed | tf_op | source)
XLA Modules:
  0.0 91.7 jit_solution(5360634306884213674)
XLA Ops:
  0.6 90.3 %shard_map.76 = (bf16[1,256,512]{2,1,0:T(8,128)(2,1)S(1)}, bf16[1,8,16384]{2,1,0:T(8,128)(2,1)S(1)}, f32[1,8,512]{2,1,0:T(8,128)S(1)}) custom-call(bf16[1,256,16384]{2,1,0:T(8,128)(2,1)} %a_hbm.1, bf16[1,256,512]{2,1,0:T(8,128)(2,1)} %l_hbm.1, s32[32]{0:T(128)} %bitcast.2, s32[32]{0:T(128)} %bitcast.3, f32[1,8,512]{2,1,0:T(8,128)} %dinv_hbm.1), custom_call_target="tpu_custom_call" | custom-call | tf_op jit(solution)/shard_map/pallas_call | solution.py:364
  90.9 0.8 shard_map.77

commit v6 on v5

--- a/solution.py
+++ b/solution.py
@@ -327,12 +327,15 @@
             src_ref=arrived, dst_ref=arrived, send_sem=turn_send.at[0], recv_sem=turn_recv.at[plane],
             device_id=(sibling, here), device_id_type=MESH,
         ).wait_recv()
+        columns = pl.ds(pl.multiple_of(plane * (PLANE * ROWS), B), PLANE * ROWS)
+        parts = []
         for i in range(PLANE // NY):
             number = plane * (PLANE // NY) + i
-            columns = pl.ds(pl.multiple_of(number * B, B), B)
+            block = pl.ds(pl.multiple_of(number * B, B), B)
             keep = jnp.full((B // NGRID, B), mask_ref[number], jnp.int32) == 1
-            left = jnp.where(keep, rows_in[:, columns], jnp.zeros((), jnp.bfloat16))
-            update += jnp.dot(left, whole[columns, :], preferred_element_type=jnp.float32)
+            parts.append(jnp.where(keep, rows_in[:, block], jnp.zeros((), jnp.bfloat16)))
+        left = jnp.concatenate(parts, axis=1)
+        update += jnp.dot(left, whole[columns, :], preferred_element_type=jnp.float32)
     small[2].wait()
     diag_ref[0] = dinv_ref[...] - update
 

time: 92.5 us -> 92.5 us (level)
  no operation moved by 1% of the time
where the time goes in v6:
time: 92.5 us; the launch traced here: 91.7 us
  Pallas kernels  91.1 us (98%)
    pallas_call x1, Pallas kernels, body(): pl.pallas_call(kernel, out_shape=tuple((pltpu.VMEM(*shape) for shape in s...  90.3 us

profile of v6, /device:TPU:8, one launch (start us, length us, event | category | flops | bytes accessed | tf_op | source)
XLA Modules:
  0.0 91.7 jit_solution(4085287451316034107)
XLA Ops:
  0.6 90.3 %shard_map.76 = (bf16[1,256,512]{2,1,0:T(8,128)(2,1)S(1)}, bf16[1,8,16384]{2,1,0:T(8,128)(2,1)S(1)}, f32[1,8,512]{2,1,0:T(8,128)S(1)}) custom-call(bf16[1,256,16384]{2,1,0:T(8,128)(2,1)} %a_hbm.1, bf16[1,256,512]{2,1,0:T(8,128)(2,1)} %l_hbm.1, s32[32]{0:T(128)} %bitcast.2, s32[32]{0:T(128)} %bitcast.3, f32[1,8,512]{2,1,0:T(8,128)} %dinv_hbm.1), custom_call_target="tpu_custom_call" | custom-call | tf_op jit(solution)/shard_map/pallas_call | solution.py:367
  90.9 0.8 shard_map.77
